TPU v7x, 32 devices: a whole 2x2x4 slice. The times are simulated.
32 devices in a mesh: mem: 8 (over z, y), hz: 4 (over x, core).
Axes of the slice: x: 2, y: 2, z: 4, core: 2. Of those that a mesh axis runs over, the one named last changes fastest.
Arguments:
- prior: float32 [8, 64, 32768], P('mem', None, 'hz'), may hold values from -6 to 6
- posterior: float32 [8, 64, 32768], P('mem', None, 'hz'), may hold values from -4 to 4
- control: float32 [64, 32768], P(None, 'hz'), may hold values from -6 to 6
- relax: float32 [64], replicated, may hold values from 0.5 to 0.95
- ocean: int32 [32768], P('hz'), may hold values 0 or 1
Outputs:
- analysis: float32 [8, 64, 32768], P('mem', None, 'hz')
All inputs are finite; a program needn't handle non-finite values. No bound on the sum of `ocean` on one device may be relied on, other than what follows from the above.
Results may differ from a plain program's by a relative error of at most 0.00002.
Values sent between devices are 32-bit elements; how exact they have to be, the bound alone decides.
A program may use at most 64 MiB of HBM per device.

v0:
```python
import functools

import jax
import jax.numpy as jnp
from jax import lax
from jax.experimental import pallas as pl
from jax.experimental.pallas import tpu as pltpu
from jax.sharding import PartitionSpec as P

eps = 1e-06
SUB = 8
LANE = 128
LAG = 2
MESH = pl.DeviceIdType.MESH
POST, PRIOR = 0, 1


def kernel(members, blocks, prior_hbm, post_hbm, control_hbm, relax_ref, ocean_ref, out_hbm,
           x, control, weights, total, out, y_in, pair, a_in, b_in, b_sum, b_swap, b_swap_prior, spread, part1, part2, zero,
           load_sem, control_sem, out_sem, y_send, y_recv, a_send, a_recv, b_send, b_recv, s_send, s_recv, p_send, p_recv,
           ga_send, ga_recv, gy_send, gy_recv, gb_send, gb_recv, h_send, h_recv, m_send, m_recv):
    levels, columns = control.shape
    half = columns // 2
    nblocks = levels // SUB
    quarter = nblocks // 4
    depth = members // 2
    m = lax.axis_index("mem")
    hz = lax.axis_index("hz")
    z = lax.div(m, 2)
    y = lax.rem(m, 2)
    other = 1 - y

    def device(zz, yy):
        return {"mem": zz * 2 + yy, "hz": hz}

    def rows(block):
        return pl.ds(pl.multiple_of(block * SUB, SUB), SUB)

    def cols(h):
        return pl.ds(pl.multiple_of(h * half, LANE), half)

    fields = (post_hbm, prior_hbm)

    def load(field, block):
        at = pl.ds(block * SUB, SUB)
        return pltpu.make_async_copy(fields[field].at[0, at], x.at[field, at], load_sem.at[field, block])

    order = []
    for i in range(2 * quarter):
        order += [i, 2 * quarter + i]
    for field in (POST, PRIOR):
        for block in order:
            load(field, block).start()
    control_load = pltpu.make_async_copy(control_hbm, control, control_sem)
    control_load.start()

    barrier = pltpu.get_barrier_semaphore()
    for i in range(1, members):
        pl.semaphore_signal(barrier, inc=1, device_id={"mem": lax.rem(m + i, members), "hz": hz}, device_id_type=MESH)
    for i in range(1, blocks):
        pl.semaphore_signal(barrier, inc=1, device_id={"mem": m, "hz": lax.rem(hz + i, blocks)}, device_id_type=MESH)
    weights[...] = jnp.broadcast_to(ocean_ref[...].astype(jnp.float32), (SUB, columns))
    spread[...] = jnp.zeros_like(spread)
    pl.semaphore_wait(barrier, members - 1 + blocks - 1)

    pending = []

    def send(src, dst, send_sem, recv_sem, to, cond=None):
        copy = pltpu.make_async_remote_copy(src_ref=src, dst_ref=dst, send_sem=send_sem, recv_sem=recv_sem,
                                            device_id=to, device_id_type=MESH)
        if cond is None:
            copy.start()
        else:
            pl.when(cond)(copy.start)
        pending.append((cond, copy))

    def arrive(dst, send_sem, recv_sem):
        pltpu.make_async_remote_copy(src_ref=dst, dst_ref=dst, send_sem=send_sem, recv_sem=recv_sem,
                                     device_id=device(z, other), device_id_type=MESH).wait_recv()

    def merge(own, n_own, came, n_came, dst, field, block, h, scale=None):
        n_own = jnp.float32(n_own)
        n_came = jnp.float32(n_came) if isinstance(n_came, int) else n_came.astype(jnp.float32)
        w = weights.at[:, cols(h)]
        acc = jnp.zeros((SUB, LANE), jnp.float32)
        for j in range(half // LANE):
            at = slice(j * LANE, (j + 1) * LANE)
            a, b = own[:, at], came[:, at]
            d = b * n_own - a * n_came
            acc += d * d * w[:, at]
            if dst is not None:
                dst[:, at] = a + b
        acc = acc / jnp.full((SUB, LANE), n_own * n_came * (n_own + n_came), jnp.float32)
        if scale is not None:
            acc = acc * scale
        spread[field, block] += acc

    up_near = 2 * z < depth
    near = jnp.where(up_near, 0, 1)
    far = 1 - near

    def place(d):
        at = jnp.where(d == 0, z, depth - 1 - z)
        return at, z + 1 - 2 * d, z - 1 + 2 * d

    def first(field):
        for block in order:
            load(field, block).wait()
        for d in (near, far):
            for k in range(quarter):
                i = d * quarter + k
                send(x.at[field, rows(i), cols(other)], y_in.at[field, i], y_send.at[field, i], y_recv.at[field, i],
                     device(z, other))

    def start_b(field):
        at, nxt, _ = place(near)
        for k in range(quarter):
            for h in range(2):
                i = near * quarter + k
                send(x.at[field, rows(2 * quarter + i), pl.ds(h * half, half)], b_in.at[field, i, h],
                     b_send.at[field, i, h], b_recv.at[field, i, h], device(nxt, y), (at == 0) & (at < depth - 1))

    def pair_step(field, d, k):
        at, nxt, _ = place(d)
        i = d * quarter + k
        mine = pair.at[field, i]
        arrive(y_in.at[field, i], y_send.at[field, i], y_recv.at[field, i])
        merge(x.at[field, rows(i), cols(y)], 1, y_in.at[field, i], 1, mine, field, i, y)
        send(mine, a_in.at[field, i], a_send.at[field, i], a_recv.at[field, i], device(nxt, y), (at == 0) & (at < depth - 1))

    def a_step(field, d, k):
        at, nxt, back = place(d)
        i = d * quarter + k
        mine = pair.at[field, i]

        @pl.when(at > 0)
        def _():
            arrive(a_in.at[field, i], a_send.at[field, i], a_recv.at[field, i])
            merge(mine, 2, a_in.at[field, i], 2 * at, mine, field, i, y)

        send(mine, a_in.at[field, i], a_send.at[field, i], a_recv.at[field, i], device(nxt, y), (at > 0) & (at < depth - 1))
        if field == POST:
            last = at == depth - 1
            spot = total.at[rows(i), cols(y)]

            @pl.when(last)
            def _():
                spot[...] = mine[...]

            send(mine, spot, ga_send.at[i], ga_recv.at[i], device(back, y), last & (at > 0))
            send(mine, spot, gy_send.at[i], gy_recv.at[i], device(z, other), last)

    def b_step(field, d, k, h):
        at, nxt, _ = place(d)
        i = d * quarter + k
        block = 2 * quarter + i
        own = x.at[field, rows(block), cols(h)]
        mine = b_sum.at[field, i, h]

        @pl.when(at > 0)
        def _():
            arrive(b_in.at[field, i, h], b_send.at[field, i, h], b_recv.at[field, i, h])
            merge(own, 1, b_in.at[field, i, h], at, mine, field, block, h)

        last = at == depth - 1
        send(mine, b_in.at[field, i, h], b_send.at[field, i, h], b_recv.at[field, i, h], device(nxt, y), (at > 0) & ~last)
        if field == POST:
            send(mine, b_swap.at[i, h], s_send.at[i, h], s_recv.at[i, h], device(z, other), last)
        else:
            send(mine, b_swap_prior.at[i], p_send.at[i], p_recv.at[i], device(z, other), last & (other == h))

    def swap_step(d, k, h):
        at, _, back = place(d)
        i = d * quarter + k
        block = 2 * quarter + i
        last = at == depth - 1
        spot = total.at[rows(block), pl.ds(h * half, half)]

        @pl.when(last)
        def _():
            arrive(b_swap.at[i, h], s_send.at[i, h], s_recv.at[i, h])
            merge(b_sum.at[POST, i, h], depth, b_swap.at[i, h], depth, spot, POST, block, h, jnp.where(y == h, 1.0, 0.0))

        send(spot, spot, gb_send.at[i, h], gb_recv.at[i, h], device(back, y), last & (at > 0))

    def swap_prior(d, k):
        at, _, _ = place(d)
        i = d * quarter + k

        @pl.when(at == depth - 1)
        def _():
            arrive(b_swap_prior.at[i], p_send.at[i], p_recv.at[i])
            merge(b_sum.at[PRIOR, i, y], depth, b_swap_prior.at[i], depth, None, PRIOR, 2 * quarter + i, y)

    def a_relay(d, k):
        at, _, back = place(d)
        i = d * quarter + k
        spot = total.at[rows(i), cols(y)]
        below = at < depth - 1

        @pl.when(below)
        def _():
            arrive(spot, ga_send.at[i], ga_recv.at[i])

        send(spot, spot, ga_send.at[i], ga_recv.at[i], device(back, y), below & (at > 0))
        send(spot, spot, gy_send.at[i], gy_recv.at[i], device(z, other), below)

    def b_relay(d, k, h):
        at, _, back = place(d)
        i = d * quarter + k
        spot = total.at[rows(2 * quarter + i), pl.ds(h * half, half)]
        below = at < depth - 1

        @pl.when(below)
        def _():
            arrive(spot, gb_send.at[i, h], gb_recv.at[i, h])

        send(spot, spot, gb_send.at[i, h], gb_recv.at[i, h], device(back, y), below & (at > 0))

    first(POST)
    start_b(POST)
    first(PRIOR)

    def chain(field):
        steps = []
        for k in range(quarter):
            for h in range(2):
                steps.append(functools.partial(lambda k, h, d: b_step(field, d, k, h), k, h))
        for k in range(quarter):
            steps.append(functools.partial(lambda k, d: a_step(field, d, k), k))
        return steps

    post_steps, prior_steps = chain(POST), chain(PRIOR)
    nb = 2 * quarter
    pairs = [(field, d, k) for field in (POST, PRIOR) for d in (near, far) for k in range(quarter)]
    swaps = [functools.partial(lambda k, h, d: swap_step(d, k, h), k, h) for k in range(quarter) for h in range(2)]
    steps = post_steps + prior_steps
    n = len(steps)
    units = [(None, k) for k in range(quarter)] + [(h, k) for k in range(quarter) for h in range(2)]

    def relay(d, h, k):
        if h is None:
            a_relay(d, k)
        else:
            b_relay(d, k, h)

    events = []
    for u in range(len(units) + 1):
        if u < len(units):
            events.append((far, *units[u]))
        if u >= 1:
            events.append((near, *units[u - 1]))
    cut1, cut2 = len(events) // 3, 2 * len(events) // 3
    done_pairs = 0
    for s in range(n + LAG):
        if done_pairs < len(pairs):
            pair_step(*pairs[done_pairs])
            done_pairs += 1
            if done_pairs == quarter:
                start_b(PRIOR)
        if s < n:
            steps[s](near)
        if s >= LAG:
            steps[s - LAG](far)
        t = s - LAG - nb - 1
        if 0 <= t < len(swaps):
            swaps[t](0)
            swaps[t](1)
        if s == n + LAG - 2:
            relay(*events[0])
    for k in range(quarter):
        swap_prior(0, k)
        swap_prior(1, k)

    lane = lax.broadcasted_iota(jnp.int32, (SUB, LANE), 1)
    for field in (POST, PRIOR):
        packed = jnp.zeros((SUB, LANE), jnp.float32)
        for block in range(nblocks):
            packed = jnp.where(lane == block, jnp.sum(spread[field, block], axis=1, keepdims=True), packed)
        part1[hz, field] = packed
    for i in range(1, blocks):
        send(part1.at[hz], part1.at[hz], h_send.at[i], h_recv.at[hz], {"mem": m, "hz": lax.rem(hz + i, blocks)})

    for event in events[1:cut1]:
        relay(*event)
    for i in range(1, blocks):
        src = lax.rem(hz + i, blocks)
        arrive(part1.at[src], h_send.at[i], h_recv.at[src])
    for field in (POST, PRIOR):
        v = part1[0, field]
        for i in range(1, blocks):
            v = v + part1[i, field]
        part2[m, field] = v
    for i in range(1, members):
        send(part2.at[m], part2.at[m], m_send.at[i], m_recv.at[m], {"mem": lax.rem(m + i, members), "hz": hz})
    for event in events[cut1:cut2]:
        relay(*event)
    for i in range(1, members):
        src = lax.rem(m + i, members)
        arrive(part2.at[src], m_send.at[i], m_recv.at[src])
    spreads = []
    for field in (POST, PRIOR):
        v = part2[0, field]
        for i in range(1, members):
            v = v + part2[i, field]
        spreads.append(v)
    sub = lax.broadcasted_iota(jnp.int32, (SUB, LANE), 0)
    relax = jnp.zeros((SUB, LANE), jnp.float32)
    for level in range(levels):
        relax = jnp.where((sub == level % SUB) & (lane == level // SUB), relax_ref[level], relax)
    factor = relax * (jnp.sqrt((spreads[PRIOR] + eps) / (spreads[POST] + eps)) - 1.0) + 1.0
    for block in range(nblocks):
        zero[block] = jnp.broadcast_to(
            jnp.sum(jnp.where(lane == block, factor, 0.0), axis=1, keepdims=True), (SUB, LANE))
    control_load.wait()

    outs = []

    def finish(block, h):
        f = zero[block]
        c, p, t, o = (r.at[rows(block), cols(h)] for r in (control, x.at[POST], total, out))
        for j in range(half // LANE):
            at = slice(j * LANE, (j + 1) * LANE)
            o[:, at] = c[:, at] + f * (p[:, at] - t[:, at] / members)
        copy = pltpu.make_async_copy(o, out_hbm.at[0, rows(block), cols(h)], out_sem.at[block, h])
        copy.start()
        outs.append(copy)

    for i, (d, h, k) in enumerate(events):
        if i >= cut2:
            relay(d, h, k)
        if h is None:
            finish(d * quarter + k, y)
        else:
            finish(2 * quarter + d * quarter + k, h)
    for k in range(quarter):
        for d in (near, far):
            i = d * quarter + k
            arrive(total.at[rows(i), cols(other)], gy_send.at[i], gy_recv.at[i])
            finish(i, other)
    for cond, copy in pending:
        if cond is None:
            copy.wait_send()
        else:
            pl.when(cond)(copy.wait_send)
    for copy in outs:
        copy.wait()


def solution(mesh):
    members, blocks = mesh.shape["mem"], mesh.shape["hz"]

    def on_device(prior, posterior, control, relax, ocean):
        levels, columns = control.shape
        half, nblocks = columns // 2, levels // SUB
        a, q = nblocks // 2, nblocks // 4
        vmem = lambda *shape: pltpu.VMEM(shape, jnp.float32)
        dma = lambda *shape: pltpu.SemaphoreType.DMA(shape)
        hbm = pl.BlockSpec(memory_space=pl.ANY)
        return pl.pallas_call(
            functools.partial(kernel, members, blocks),
            out_shape=jax.ShapeDtypeStruct(posterior.shape, jnp.float32),
            in_specs=[hbm, hbm, hbm, pl.BlockSpec(memory_space=pltpu.SMEM), pl.BlockSpec(memory_space=pltpu.VMEM)],
            out_specs=hbm,
            scratch_shapes=[
                vmem(2, levels, columns), vmem(levels, columns), vmem(SUB, columns), vmem(levels, columns),
                vmem(levels, columns), vmem(2, a, SUB, half), vmem(2, a, SUB, half), vmem(2, a, SUB, half),
                vmem(2, a, 2, SUB, half), vmem(2, a, 2, SUB, half), vmem(a, 2, SUB, half), vmem(a, SUB, half),
                vmem(2, nblocks, SUB, LANE), vmem(blocks, 2, SUB, LANE), vmem(members, 2, SUB, LANE),
                vmem(nblocks, SUB, LANE),
                dma(2, nblocks), pltpu.SemaphoreType.DMA, dma(nblocks, 2),
                dma(2, a), dma(2, a), dma(2, a), dma(2, a), dma(2, a, 2), dma(2, a, 2), dma(a, 2), dma(a, 2), dma(a), dma(a),
                dma(a), dma(a), dma(a), dma(a), dma(a, 2), dma(a, 2), dma(blocks), dma(blocks), dma(members), dma(members),
            ],
            compiler_params=pltpu.CompilerParams(
                collective_id=0, has_side_effects=True, vmem_limit_bytes=60 * 2**20
            ),
        )(prior, posterior, control, relax, ocean.reshape(1, columns))

    return jax.shard_map(
        on_device,
        mesh=mesh,
        in_specs=(P("mem", None, "hz"), P("mem", None, "hz"), P(None, "hz"), P(), P("hz")),
        out_specs=P("mem", None, "hz"),
        check_vma=False,
    )
```

profile of v0, /device:TPU:0, one launch (start us, length us, event | category | flops | bytes accessed | tf_op | source)
XLA Modules:
  0.0 76.2 jit_solution(3117724771981400080)
XLA Ops:
  0.0 73.1 %shard_map.55 = f32[1,64,8192]{2,1,0:T(8,128)} custom-call(f32[1,64,8192]{2,1,0:T(8,128)} %prior_hbm.1, f32[1,64,8192]{2,1,0:T(8,128)} %post_hbm.1, f32[64,8192]{1,0:T(8,128)} %control_hbm.1, f32[64]{0:T(128)} %relax_ref.1, s32[1,8192]{1,0:T(1,128)} %bitcast.1), custom_call_target="tpu_custom_call" | custom-call | tf_op jit(solution)/shard_map/pallas_call | solution.py:360
  73.1 3.1 %copy.7 = f32[1,64,8192]{2,1,0:T(8,128)} copy(f32[1,64,8192]{2,1,0:T(8,128)} %shard_map.55) | data formatting | bytes 4194304
where the time goes:
time: 76.4 us; the launch traced here: 76.2 us
  Pallas kernels  73.1 us (96%)
  local copies, waits for them, and re-layouts  3.06 us (4%)
    pallas_call x1, Pallas kernels, on_device(): pl.pallas_call(functools.partial(kernel, members, blocks), out_shape=jax....  73.1 us
    unnamed x1, local copies, waits for them, and re-layouts  3.06 us

commit v1 on v0

--- a/solution.py
+++ b/solution.py
@@ -15,9 +15,9 @@
 POST, PRIOR = 0, 1
 
 
-def kernel(members, blocks, prior_hbm, post_hbm, control_hbm, relax_ref, ocean_ref, out_hbm,
-           x, control, weights, total, out, y_in, pair, a_in, b_in, b_sum, b_swap, b_swap_prior, spread, part1, part2, zero,
-           load_sem, control_sem, out_sem, y_send, y_recv, a_send, a_recv, b_send, b_recv, s_send, s_recv, p_send, p_recv,
+def kernel(members, blocks, prior_hbm, post_hbm, control_hbm, relax_hbm, ocean_hbm, out,
+           x, control, ocean, relax_ref, weights, total, y_in, pair, a_in, b_in, b_sum, b_swap, b_swap_prior, spread, part1, part2, zero,
+           load_sem, control_sem, ocean_sem, relax_sem, y_send, y_recv, a_send, a_recv, b_send, b_recv, s_send, s_recv, p_send, p_recv,
            ga_send, ga_recv, gy_send, gy_recv, gb_send, gb_recv, h_send, h_recv, m_send, m_recv):
     levels, columns = control.shape
     half = columns // 2
@@ -45,6 +45,21 @@
         at = pl.ds(block * SUB, SUB)
         return pltpu.make_async_copy(fields[field].at[0, at], x.at[field, at], load_sem.at[field, block])
 
+    barrier = pltpu.get_barrier_semaphore()
+
+    def greet(to):
+        pl.semaphore_signal(barrier, inc=1, device_id=to, device_id_type=MESH)
+
+    greet(device(z, other))
+    pl.when(z > 0)(lambda: greet(device(z - 1, y)))
+    pl.when(z < depth - 1)(lambda: greet(device(z + 1, y)))
+    for i in range(1, blocks):
+        greet({"mem": m, "hz": lax.rem(hz + i, blocks)})
+
+    ocean_load = pltpu.make_async_copy(ocean_hbm, ocean, ocean_sem)
+    ocean_load.start()
+    relax_load = pltpu.make_async_copy(relax_hbm, relax_ref, relax_sem)
+    relax_load.start()
     order = []
     for i in range(2 * quarter):
         order += [i, 2 * quarter + i]
@@ -54,14 +69,10 @@
     control_load = pltpu.make_async_copy(control_hbm, control, control_sem)
     control_load.start()
 
-    barrier = pltpu.get_barrier_semaphore()
-    for i in range(1, members):
-        pl.semaphore_signal(barrier, inc=1, device_id={"mem": lax.rem(m + i, members), "hz": hz}, device_id_type=MESH)
-    for i in range(1, blocks):
-        pl.semaphore_signal(barrier, inc=1, device_id={"mem": m, "hz": lax.rem(hz + i, blocks)}, device_id_type=MESH)
-    weights[...] = jnp.broadcast_to(ocean_ref[...].astype(jnp.float32), (SUB, columns))
+    ocean_load.wait()
+    weights[...] = jnp.broadcast_to(ocean[...].astype(jnp.float32), (SUB, columns))
     spread[...] = jnp.zeros_like(spread)
-    pl.semaphore_wait(barrier, members - 1 + blocks - 1)
+    pl.semaphore_wait(barrier, blocks + jnp.where(z > 0, 1, 0) + jnp.where(z < depth - 1, 1, 0))
 
     pending = []
 
@@ -305,6 +316,7 @@
             v = v + part2[i, field]
         spreads.append(v)
     sub = lax.broadcasted_iota(jnp.int32, (SUB, LANE), 0)
+    relax_load.wait()
     relax = jnp.zeros((SUB, LANE), jnp.float32)
     for level in range(levels):
         relax = jnp.where((sub == level % SUB) & (lane == level // SUB), relax_ref[level], relax)
@@ -314,17 +326,12 @@
             jnp.sum(jnp.where(lane == block, factor, 0.0), axis=1, keepdims=True), (SUB, LANE))
     control_load.wait()
 
-    outs = []
-
     def finish(block, h):
         f = zero[block]
-        c, p, t, o = (r.at[rows(block), cols(h)] for r in (control, x.at[POST], total, out))
+        c, p, t, o = (r.at[rows(block), cols(h)] for r in (control, x.at[POST], total, out.at[0]))
         for j in range(half // LANE):
             at = slice(j * LANE, (j + 1) * LANE)
             o[:, at] = c[:, at] + f * (p[:, at] - t[:, at] / members)
-        copy = pltpu.make_async_copy(o, out_hbm.at[0, rows(block), cols(h)], out_sem.at[block, h])
-        copy.start()
-        outs.append(copy)
 
     for i, (d, h, k) in enumerate(events):
         if i >= cut2:
@@ -343,8 +350,6 @@
             copy.wait_send()
         else:
             pl.when(cond)(copy.wait_send)
-    for copy in outs:
-        copy.wait()
 
 
 def solution(mesh):
@@ -356,19 +361,19 @@
         a, q = nblocks // 2, nblocks // 4
         vmem = lambda *shape: pltpu.VMEM(shape, jnp.float32)
         dma = lambda *shape: pltpu.SemaphoreType.DMA(shape)
-        hbm = pl.BlockSpec(memory_space=pl.ANY)
+        hbm = pl.BlockSpec(memory_space=pltpu.HBM)
         return pl.pallas_call(
             functools.partial(kernel, members, blocks),
-            out_shape=jax.ShapeDtypeStruct(posterior.shape, jnp.float32),
-            in_specs=[hbm, hbm, hbm, pl.BlockSpec(memory_space=pltpu.SMEM), pl.BlockSpec(memory_space=pltpu.VMEM)],
-            out_specs=hbm,
+            out_shape=pltpu.VMEM(posterior.shape, jnp.float32),
+            in_specs=[hbm] * 5,
+            out_specs=pl.BlockSpec(memory_space=pltpu.VMEM),
             scratch_shapes=[
-                vmem(2, levels, columns), vmem(levels, columns), vmem(SUB, columns), vmem(levels, columns),
-                vmem(levels, columns), vmem(2, a, SUB, half), vmem(2, a, SUB, half), vmem(2, a, SUB, half),
+                vmem(2, levels, columns), vmem(levels, columns), pltpu.VMEM((1, columns), jnp.int32),
+                pltpu.SMEM((levels,), jnp.float32), vmem(SUB, columns), vmem(levels, columns), vmem(2, a, SUB, half), vmem(2, a, SUB, half), vmem(2, a, SUB, half),
                 vmem(2, a, 2, SUB, half), vmem(2, a, 2, SUB, half), vmem(a, 2, SUB, half), vmem(a, SUB, half),
                 vmem(2, nblocks, SUB, LANE), vmem(blocks, 2, SUB, LANE), vmem(members, 2, SUB, LANE),
                 vmem(nblocks, SUB, LANE),
-                dma(2, nblocks), pltpu.SemaphoreType.DMA, dma(nblocks, 2),
+                dma(2, nblocks), pltpu.SemaphoreType.DMA, pltpu.SemaphoreType.DMA, pltpu.SemaphoreType.DMA,
                 dma(2, a), dma(2, a), dma(2, a), dma(2, a), dma(2, a, 2), dma(2, a, 2), dma(a, 2), dma(a, 2), dma(a), dma(a),
                 dma(a), dma(a), dma(a), dma(a), dma(a, 2), dma(a, 2), dma(blocks), dma(blocks), dma(members), dma(members),
             ],

time: 76.4 us -> 73.5 us (0.962)
  local copies, waits for them, and re-layouts: 3.06 us -> 1.32 us
  Pallas kernels: 73.1 us -> 72 us
    unnamed x1, local copies, waits for them, and re-layouts: 3.06 us -> 1.32 us
    pallas_call x1, Pallas kernels: 73.1 us -> 72 us  [on_device(): pl.pallas_call(functools.partial(kernel, members, blocks), out_shape=pltp...]
where the time goes in v1:
time: 73.5 us; the launch traced here: 73.3 us
  Pallas kernels  72 us (98%)
  local copies, waits for them, and re-layouts  1.32 us (2%)
    pallas_call x1, Pallas kernels, on_device(): pl.pallas_call(functools.partial(kernel, members, blocks), out_shape=pltp...  72 us

profile of v1, /device:TPU:0, one launch (start us, length us, event | category | flops | bytes accessed | tf_op | source)
XLA Modules:
  0.0 73.3 jit_solution(10400826233483689359)
XLA Ops:
  0.0 72.0 %shard_map.55 = f32[1,64,8192]{2,1,0:T(8,128)S(1)} custom-call(f32[1,64,8192]{2,1,0:T(8,128)} %prior_hbm.1, f32[1,64,8192]{2,1,0:T(8,128)} %post_hbm.1, f32[64,8192]{1,0:T(8,128)} %control_hbm.1, f32[64]{0:T(128)} %relax_hbm.1, s32[1,8192]{1,0:T(1,128)} %bitcast.1), custom_call_target="tpu_custom_call" | custom-call | tf_op jit(solution)/shard_map/pallas_call | solution.py:365
  72.0 1.3 %copy.7 = f32[1,64,8192]{2,1,0:T(8,128)} copy(f32[1,64,8192]{2,1,0:T(8,128)S(1)} %shard_map.55) | data formatting | bytes 4194304

commit v2 on v1

v2 whole, which is shorter than its diff:
```python
import functools

import jax
import jax.numpy as jnp
from jax import lax
from jax.experimental import pallas as pl
from jax.experimental.pallas import tpu as pltpu
from jax.sharding import PartitionSpec as P

eps = 1e-06
SUB = 8
LANE = 128
MESH = pl.DeviceIdType.MESH
POST, PRIOR = 0, 1
ROWS_FIRST, DEPTH_FIRST = 0, 1
NEAR, FAR = 0, 1
PAIRS = 4
SHARE = 0.34375

(Y_SEND, Y_RECV, RS_IN, RS_OUT, RS_FROM_OUT, RS_FROM_IN, SW_SEND, SW_RECV,
 AG_IN, AG_OUT, AG_FROM_OUT, AG_FROM_IN, AGY_SEND, AGY_RECV, STAT1, STAT2, STAT3) = range(17)

MIDDLE = ((0, 1, 2), (0, 1, 3), (1, 0, 2))
ORDER_END = (
    0, 73, 91, 3, 77, 1, 32, 89, 2, 35, 67, 6, 33, 65, 5, 34, 76, 168, 200, 38, 95, 4, 186, 37, 69, 7, 232, 93, 184, 23,
    36, 75, 17, 162, 39, 71, 218, 160, 55, 87, 216, 19, 49, 81, 190, 250, 16, 248, 78, 364, 222, 51, 83, 386, 164, 48,
    260, 22, 188, 254, 79, 170, 202, 418, 256, 21, 365, 54, 220, 166, 262, 234, 20, 258, 182, 53, 388, 252, 85, 176, 18,
    52, 84, 384, 420, 266, 357, 389, 50, 178, 448, 264, 353, 385, 416, 359, 391, 421, 355, 387, 417, 480, 366, 390, 423,
    367, 419, 512, 363, 422, 361,
)
ORDER_INNER = (
    0, 3, 1, 137, 73, 32, 2, 155, 91, 35, 141, 77, 6, 168, 104, 33, 153, 89, 5, 186, 122, 34, 131, 67, 4, 38, 184, 120,
    129, 65, 7, 37, 140, 172, 162, 98, 23, 36, 159, 95, 160, 96, 204, 39, 133, 69, 17, 55, 157, 93, 190, 126, 19, 236,
    300, 139, 75, 164, 16, 49, 100, 268, 135, 188, 22, 51, 71, 124, 151, 170, 21, 48, 106, 87, 365, 145, 20, 301, 54,
    81, 142, 166, 18, 102, 53, 147, 83, 182, 118, 52, 324, 388, 260, 176, 112, 50, 143, 79, 178, 114, 320, 384, 256,
    420, 357, 293, 389, 326, 262, 174, 206, 416, 322, 258, 353, 289, 386, 421, 149, 85, 359, 295, 391, 238, 270, 148,
    355, 291, 387, 302, 418, 330, 266, 180, 448, 385, 328, 264, 423, 367, 303, 480, 390, 363, 299, 419, 361, 297, 417,
    512, 422,
)


def decode(step):
    step, side = divmod(step, 2)
    step, k = divmod(step, PAIRS)
    step, cls = divmod(step, 2)
    op, field = divmod(step, 2)
    return op, field, cls, k, side


def when(cond, do):
    if isinstance(cond, bool):
        if cond:
            do()
    else:
        pl.when(cond)(do)


def kernel(members, blocks, wide, prior_hbm, post_hbm, control_hbm, relax_hbm, ocean_hbm, out,
           x, control, ocean, relax_ref, weights, total, y_in, a_sum, a_in, b_sum, b_in, b_swap, spread, part1, part2, factors,
           load_sem, control_sem, ocean_sem, relax_sem, y_send, y_recv, a_send, a_recv, b_send, b_recv, w_send, w_recv,
           ga_send, ga_recv, gb_send, gb_recv, gy_send, gy_recv, h_send, h_recv, m_send, m_recv):
    levels, columns = control.shape
    nblocks = levels // SUB
    pairs = nblocks // 2
    rest = columns - 2 * wide
    half = rest // 2
    depth = members // 2
    m = lax.axis_index("mem")
    hz = lax.axis_index("hz")
    z = lax.div(m, 2)
    y = lax.rem(m, 2)
    other = 1 - y
    upper = z >= depth // 2
    up = jnp.where(upper, 1, 0)
    inward = jnp.where(upper, z - 1, z + 1)
    outward = jnp.where(upper, z + 1, z - 1)
    distance = jnp.where(upper, depth - 1 - z, z)
    center = depth // 2 - 1
    to_in, to_out = up, 1 - up

    def device(zz, yy):
        return {"mem": zz * 2 + yy, "hz": hz}

    barrier = pltpu.get_barrier_semaphore()

    def greet(to):
        pl.semaphore_signal(barrier, inc=1, device_id=to, device_id_type=MESH)

    greet(device(z, other))
    greet(device(inward, y))
    pl.when(distance > 0)(lambda: greet(device(outward, y)))
    for i in range(1, blocks):
        greet({"mem": m, "hz": lax.rem(hz + i, blocks)})

    def block_of(k, side):
        return k + pairs * (up if side == NEAR else 1 - up)

    def rows(block):
        return pl.ds(pl.multiple_of(block * SUB, SUB), SUB)

    def wide_cols(yy):
        return pl.ds(pl.multiple_of(yy * wide, LANE), wide)

    rest_cols = pl.ds(2 * wide, rest)
    fields = (post_hbm, prior_hbm)

    def load(field, block):
        return pltpu.make_async_copy(fields[field].at[0, rows(block)], x.at[field, rows(block)], load_sem.at[field, block])

    for field in (POST, PRIOR):
        for k in range(pairs):
            for side in (FAR, NEAR):
                load(field, block_of(k, side)).start()
    ocean_load = pltpu.make_async_copy(ocean_hbm, ocean, ocean_sem)
    ocean_load.start()
    control_load = pltpu.make_async_copy(control_hbm, control, control_sem)
    control_load.start()
    relax_load = pltpu.make_async_copy(relax_hbm, relax_ref, relax_sem)
    relax_load.start()
    spread[...] = jnp.zeros_like(spread)
    ocean_load.wait()
    weights[...] = jnp.broadcast_to(ocean[...].astype(jnp.float32), (SUB, columns))
    pl.semaphore_wait(barrier, 1 + blocks + jnp.where(distance > 0, 1, 0))

    def arrive(dst, send_sem, recv_sem):
        pltpu.make_async_remote_copy(src_ref=dst, dst_ref=dst, send_sem=send_sem, recv_sem=recv_sem,
                                     device_id=device(z, other), device_id_type=MESH).wait_recv()

    def merge(own, n_own, came, n_came, w, dst, field, block, scale=1.0):
        acc = jnp.zeros((SUB, LANE), jnp.float32)
        static = isinstance(n_own, int) and isinstance(n_came, int)
        equal = static and n_own == n_came
        if not static:
            f_own, f_came = (jnp.float32(n) if isinstance(n, int) else n.astype(jnp.float32) for n in (n_own, n_came))
        for j in range(own.shape[-1] // LANE):
            at = slice(j * LANE, (j + 1) * LANE)
            a, b = own[:, at], came[:, at]
            if equal:
                d = b - a
            elif static:
                d = b * float(n_own) - a * float(n_came)
            else:
                d = b * f_own - a * f_came
            acc += d * d * w[:, at]
            if dst is not None:
                dst[:, at] = a + b
        if equal:
            acc = acc * (scale / (2 * n_own))
        elif static:
            acc = acc * (scale / (n_own * n_came * (n_own + n_came)))
        else:
            acc = acc / jnp.full((SUB, LANE), f_own * f_came * (f_own + f_came), jnp.float32) * scale
        spread[field, block] += acc

    lane = lax.broadcasted_iota(jnp.int32, (SUB, LANE), 1)
    sub = lax.broadcasted_iota(jnp.int32, (SUB, LANE), 0)

    def role(order, end):
        pending = []
        loaded = set()
        finished = []
        state = {"factor": False}
        far = 0 if end else (1 if center == 1 else distance)
        at_center = False if end else (True if center == 1 else distance == center)
        before = False if end else (False if center == 1 else distance < center)
        last_step = {}
        for i, step in enumerate(order):
            op, *chunk = decode(step)
            if op in (AG_OUT, AGY_SEND):
                last_step[tuple(chunk)] = i

        def send(src, dst, send_sem, recv_sem, to, cond=True):
            copy = pltpu.make_async_remote_copy(src_ref=src, dst_ref=dst, send_sem=send_sem, recv_sem=recv_sem,
                                                device_id=to, device_id_type=MESH)
            when(cond, copy.start)
            pending.append((cond, copy))

        def local(field, k, side):
            block = block_of(k, side)
            if (field, k, side) not in loaded:
                loaded.add((field, k, side))
                load(field, block).wait()
            return block

        def chain_send(field, cls, k, side, direction, to, cond=True):
            block = local(field, k, side)
            if cls == ROWS_FIRST:
                src, came, send_sem, recv_sem = a_sum.at[field, block], a_in, a_send, a_recv
            else:
                first = end and (side == FAR or (field, cls, k) in MIDDLE)
                src = x.at[field, rows(block), rest_cols] if first else b_sum.at[field, block]
                came, send_sem, recv_sem = b_in, b_send, b_recv
            at = (field, block, direction)
            send(src, came.at[at], send_sem.at[at], recv_sem.at[at], to, cond)

        def chain_merge(field, cls, k, side, direction, n_before, n_came, dst=True):
            block = local(field, k, side)
            at = (field, block, direction)
            if cls == ROWS_FIRST:
                came, own, w = a_in, a_sum.at[field, block], weights.at[:, wide_cols(y)]
                arrive(came.at[at], a_send.at[at], a_recv.at[at])
                into = {True: own, None: None, "total": total.at[rows(block), wide_cols(y)]}[dst]
                merge(own, 2 * n_before, came.at[at], 2 * n_came, w, into, field, block)
            else:
                came, w = b_in, weights.at[:, rest_cols]
                own = x.at[field, rows(block), rest_cols] if isinstance(n_before, int) and n_before == 1 else b_sum.at[field, block]
                arrive(came.at[at], b_send.at[at], b_recv.at[at])
                merge(own, n_before, came.at[at], n_came, w, b_sum.at[field, block], field, block)

        def spot(cls, block):
            return total.at[rows(block), wide_cols(y) if cls == ROWS_FIRST else rest_cols]

        def total_send(cls, block, direction, to, cond=True):
            s, r = (ga_send, ga_recv) if cls == ROWS_FIRST else (gb_send, gb_recv)
            at = (block, direction)
            send(spot(cls, block), spot(cls, block), s.at[at], r.at[at], to, cond)

        def total_arrive(cls, block, direction):
            s, r = (ga_send, ga_recv) if cls == ROWS_FIRST else (gb_send, gb_recv)
            at = (block, direction)
            arrive(spot(cls, block), s.at[at], r.at[at])

        def finish(block, cols):
            f = factors[block]
            c, p, t, o = (r.at[rows(block), cols] for r in (control, x.at[POST], total, out.at[0]))
            for j in range(c.shape[-1] // LANE):
                at = slice(j * LANE, (j + 1) * LANE)
                o[:, at] = c[:, at] + f * (p[:, at] - t[:, at] / members)

        def ready(block, cols):
            if state["factor"]:
                finish(block, cols)
            else:
                finished.append((block, cols))

        for i, step in enumerate(order):
            op, field, cls, k, side = decode(step)
            middle = (field, cls, k) in MIDDLE
            dst_total = "total" if cls == ROWS_FIRST and field == POST else None
            if op < STAT1:
                block = block_of(k, side)
                root_here = side == NEAR and (end != middle)
            if op == Y_SEND:
                local(field, k, side)
                send(x.at[field, rows(block), wide_cols(other)], y_in.at[field, block],
                     y_send.at[field, block], y_recv.at[field, block], device(z, other))
            elif op == Y_RECV:
                local(field, k, side)
                arrive(y_in.at[field, block], y_send.at[field, block], y_recv.at[field, block])
                merge(x.at[field, rows(block), wide_cols(y)], 1, y_in.at[field, block], 1, weights.at[:, wide_cols(y)],
                      a_sum.at[field, block], field, block)
            elif op == RS_IN:
                chain_send(field, cls, k, side, to_in, device(inward, y))
            elif op == RS_OUT:
                chain_send(field, cls, k, side, to_out, device(outward, y))
            elif op == RS_FROM_OUT:
                if side == FAR or not middle:
                    chain_merge(field, cls, k, side, to_in, 1, far)
                else:
                    chain_merge(field, cls, k, side, to_in, 1, far)
                    if before is not False:
                        chain_send(field, cls, k, side, to_in, device(inward, y), before)
            elif op == RS_FROM_IN:
                if end:
                    chain_merge(field, cls, k, side, to_out, 1, depth - 1, dst_total if cls == ROWS_FIRST else True)
                elif not middle:
                    chain_merge(field, cls, k, side, to_out, 1, depth - 1 - far)
                else:
                    when(at_center, lambda: chain_merge(field, cls, k, side, to_out, far + 1, depth - 1 - far,
                                                        dst_total if cls == ROWS_FIRST else True))
                if cls == ROWS_FIRST and field == POST and root_here and before is False:
                    ready(block, wide_cols(y))
            elif op == SW_SEND:
                cond = True if end else at_center
                if field == POST:
                    send(b_sum.at[POST, block], b_swap.at[POST, block], w_send.at[POST, block], w_recv.at[POST, block],
                         device(z, other), cond)
                else:
                    send(b_sum.at[PRIOR, block, :, pl.ds(pl.multiple_of(other * half, LANE), half)],
                         b_swap.at[PRIOR, block, :, pl.ds(0, half)],
                         w_send.at[PRIOR, block], w_recv.at[PRIOR, block], device(z, other), cond)
            elif op == SW_RECV:
                cond = True if end else at_center
                if field == POST:
                    def do(block=block):
                        arrive(b_swap.at[POST, block], w_send.at[POST, block], w_recv.at[POST, block])
                        merge(b_sum.at[POST, block], depth, b_swap.at[POST, block], depth, weights.at[:, rest_cols],
                              spot(DEPTH_FIRST, block), POST, block, 0.5)
                    when(cond, do)
                    if before is False:
                        ready(block, rest_cols)
                else:
                    def do(block=block):
                        mine = pl.ds(pl.multiple_of(y * half, LANE), half)
                        came = b_swap.at[PRIOR, block, :, pl.ds(0, half)]
                        arrive(came, w_send.at[PRIOR, block], w_recv.at[PRIOR, block])
                        merge(b_sum.at[PRIOR, block, :, mine], depth, came, depth,
                              weights.at[:, pl.ds(pl.multiple_of(2 * wide + y * half, LANE), half)], None, PRIOR, block)
                    when(cond, do)
            elif op == AG_IN:
                total_send(cls, block, to_in, device(inward, y), at_center if root_here and not end else True)
            elif op in (AG_OUT, AGY_SEND):
                cond = at_center if root_here and not end else True
                if op == AG_OUT:
                    total_send(cls, block, to_out, device(outward, y), cond)
                else:
                    send(spot(cls, block), spot(cls, block), gy_send.at[block], gy_recv.at[block], device(z, other), cond)
                if root_here and before is not False and last_step[field, cls, k, side] == i:
                    def do(cls=cls, block=block):
                        total_arrive(cls, block, to_out)
                    when(before, do)
                    total_send(cls, block, to_out, device(outward, y), before)
                    if cls == ROWS_FIRST:
                        send(spot(cls, block), spot(cls, block), gy_send.at[block], gy_recv.at[block], device(z, other), before)
                    ready(block, wide_cols(y) if cls == ROWS_FIRST else rest_cols)
            elif op == AG_FROM_OUT:
                total_arrive(cls, block, to_in)
                ready(block, wide_cols(y) if cls == ROWS_FIRST else rest_cols)
            elif op == AG_FROM_IN:
                total_arrive(cls, block, to_out)
                ready(block, wide_cols(y) if cls == ROWS_FIRST else rest_cols)
            elif op == AGY_RECV:
                arrive(total.at[rows(block), wide_cols(other)], gy_send.at[block], gy_recv.at[block])
                ready(block, wide_cols(other))
            elif op == STAT1:
                for field in (POST, PRIOR):
                    packed = jnp.zeros((SUB, LANE), jnp.float32)
                    for b in range(nblocks):
                        packed = jnp.where(lane == b, jnp.sum(spread[field, b], axis=1, keepdims=True), packed)
                    part1[hz, field] = packed
                for b in range(1, blocks):
                    send(part1.at[hz], part1.at[hz], h_send.at[b], h_recv.at[hz], {"mem": m, "hz": lax.rem(hz + b, blocks)})
            elif op == STAT2:
                for b in range(1, blocks):
                    src = lax.rem(hz + b, blocks)
                    arrive(part1.at[src], h_send.at[b], h_recv.at[src])
                for field in (POST, PRIOR):
                    v = part1[0, field]
                    for b in range(1, blocks):
                        v = v + part1[b, field]
                    part2[m, field] = v
                for b in range(1, members):
                    send(part2.at[m], part2.at[m], m_send.at[b], m_recv.at[m], {"mem": lax.rem(m + b, members), "hz": hz})
            elif op == STAT3:
                for b in range(1, members):
                    src = lax.rem(m + b, members)
                    arrive(part2.at[src], m_send.at[b], m_recv.at[src])
                sums = []
                for field in (POST, PRIOR):
                    v = part2[0, field]
                    for b in range(1, members):
                        v = v + part2[b, field]
                    sums.append(v)
                relax_load.wait()
                relax = jnp.zeros((SUB, LANE), jnp.float32)
                for level in range(levels):
                    relax = jnp.where((sub == level % SUB) & (lane == level // SUB), relax_ref[level], relax)
                factor = relax * (jnp.sqrt((sums[PRIOR] + eps) / (sums[POST] + eps)) - 1.0) + 1.0
                for b in range(nblocks):
                    factors[b] = jnp.broadcast_to(
                        jnp.sum(jnp.where(lane == b, factor, 0.0), axis=1, keepdims=True), (SUB, LANE))
                control_load.wait()
                state["factor"] = True
            if state["factor"] and finished:
                for _ in range(2):
                    if finished:
                        finish(*finished.pop(0))
        for todo in finished:
            finish(*todo)
        for cond, copy in pending:
            when(cond, copy.wait_send)

    @pl.when(distance == 0)
    def _():
        role(ORDER_END, True)

    @pl.when(distance > 0)
    def _():
        role(ORDER_INNER, False)


def solution(mesh):
    members, blocks = mesh.shape["mem"], mesh.shape["hz"]

    def on_device(prior, posterior, control, relax, ocean):
        levels, columns = control.shape
        n = levels // SUB
        wide = round(columns * SHARE / LANE) * LANE
        rest = columns - 2 * wide
        vmem = lambda *shape: pltpu.VMEM(shape, jnp.float32)
        dma = lambda *shape: pltpu.SemaphoreType.DMA(shape)
        one = pltpu.SemaphoreType.DMA
        return pl.pallas_call(
            functools.partial(kernel, members, blocks, wide),
            out_shape=pltpu.VMEM(posterior.shape, jnp.float32),
            in_specs=[pl.BlockSpec(memory_space=pltpu.HBM)] * 5,
            out_specs=pl.BlockSpec(memory_space=pltpu.VMEM),
            scratch_shapes=[
                vmem(2, levels, columns), vmem(levels, columns), pltpu.VMEM((1, columns), jnp.int32),
                pltpu.SMEM((levels,), jnp.float32), vmem(SUB, columns), vmem(levels, columns),
                vmem(2, n, SUB, wide), vmem(2, n, SUB, wide), vmem(2, n, 2, SUB, wide),
                vmem(2, n, SUB, rest), vmem(2, n, 2, SUB, rest), vmem(2, n, SUB, rest),
                vmem(2, n, SUB, LANE), vmem(blocks, 2, SUB, LANE), vmem(members, 2, SUB, LANE), vmem(n, SUB, LANE),
                dma(2, n), one, one, one, dma(2, n), dma(2, n), dma(2, n, 2), dma(2, n, 2), dma(2, n, 2), dma(2, n, 2),
                dma(2, n), dma(2, n), dma(n, 2), dma(n, 2), dma(n, 2), dma(n, 2), dma(n), dma(n),
                dma(blocks), dma(blocks), dma(members), dma(members),
            ],
            compiler_params=pltpu.CompilerParams(
                collective_id=0, has_side_effects=True, vmem_limit_bytes=60 * 2**20
            ),
        )(prior, posterior, control, relax, ocean.reshape(1, columns))

    return jax.shard_map(
        on_device,
        mesh=mesh,
        in_specs=(P("mem", None, "hz"), P("mem", None, "hz"), P(None, "hz"), P(), P("hz")),
        out_specs=P("mem", None, "hz"),
        check_vma=False,
    )
```

time: 73.5 us -> 67.9 us (0.924)
  Pallas kernels: 72 us -> 66.4 us
    pallas_call x1, Pallas kernels: 72 us -> 66.4 us  [on_device(): pl.pallas_call(functools.partial(kernel, members, blocks, wide), out_shap...]
where the time goes in v2:
time: 67.9 us; the launch traced here: 67.7 us
  Pallas kernels  66.4 us (98%)
  local copies, waits for them, and re-layouts  1.32 us (2%)
    pallas_call x1, Pallas kernels, on_device(): pl.pallas_call(functools.partial(kernel, members, blocks, wide), out_shap...  66.4 us

profile of v2, /device:TPU:0, one launch (start us, length us, event | category | flops | bytes accessed | tf_op | source)
XLA Modules:
  0.0 67.7 jit_solution(1386204701202420187)
XLA Ops:
  0.0 66.4 %shard_map.55 = f32[1,64,8192]{2,1,0:T(8,128)S(1)} custom-call(f32[1,64,8192]{2,1,0:T(8,128)} %prior_hbm.1, f32[1,64,8192]{2,1,0:T(8,128)} %post_hbm.1, f32[64,8192]{1,0:T(8,128)} %control_hbm.1, f32[64]{0:T(128)} %relax_hbm.1, s32[1,8192]{1,0:T(1,128)} %bitcast.1), custom_call_target="tpu_custom_call" | custom-call | tf_op jit(solution)/shard_map/pallas_call | solution.py:393
  66.4 1.3 %copy.7 = f32[1,64,8192]{2,1,0:T(8,128)} copy(f32[1,64,8192]{2,1,0:T(8,128)S(1)} %shard_map.55) | data formatting | bytes 4194304

commit v3 on v2

v3 whole, which is shorter than its diff:
```python
import functools
import math

import jax
import jax.numpy as jnp
from jax import lax
from jax.experimental import pallas as pl
from jax.experimental.pallas import tpu as pltpu
from jax.sharding import PartitionSpec as P

eps = 1e-06
SUB = 8
LANE = 128
MESH = pl.DeviceIdType.MESH
POST, PRIOR = 0, 1
ROWS_FIRST, DEPTH_FIRST = 0, 1
NEAR, FAR = 0, 1
PAIRS = 4
SHORT_LINE = 4

(Y_SEND, Y_RECV, RS_IN, RS_OUT, RS_FROM_OUT, RS_FROM_IN, SW_SEND, SW_RECV, AG_IN, AG_OUT, AG_RECV,
 AGY_SEND, AGY_RECV, V_SEND, V_RECV, W_SEND, W_RECV, STAT1, STAT2, STAT3) = range(20)

PLAN = {
    "share": 0.375,
    "split": 1,
    "middle": ((0, 1, 1), (0, 1, 2), (0, 1, 3), (1, 0, 3)),
    "via": {(1, 0, 1): 1, (1, 1, 0): 1, (1, 1, 1): 1, (1, 2, 0): 1, (1, 2, 1): 1, (1, 3, 1): 1},
    "end": (
        181, 13, 177, 5, 157, 149, 9, 77, 929, 141, 32, 69, 936, 185, 40, 156, 73, 937, 1, 137, 96, 933, 12, 189, 104,
        941, 145, 37, 368, 148, 65, 432, 129, 932, 33, 76, 372, 133, 41, 101, 496, 165, 332, 8, 376, 97, 524, 4, 668,
        105, 169, 0, 72, 328, 520, 380, 444, 336, 400, 68, 161, 45, 669, 64, 153, 508, 320, 704, 512, 464, 324, 708,
        516, 109, 44, 173, 768, 660, 440, 436, 152, 772, 653, 717, 528, 108, 36, 172, 360, 504, 500, 649, 713, 781, 716,
        352, 100, 356, 1088, 641, 705, 777, 645, 709, 1152, 780, 712, 664, 769, 1216, 661, 657, 773, 665, 776,
    ),
    "inner": (
        865, 8, 872, 4, 873, 13, 309, 181, 72, 305, 177, 869, 12, 285, 68, 157, 877, 5, 277, 149, 372, 77, 9, 368, 240,
        269, 141, 76, 868, 313, 0, 185, 69, 284, 348, 244, 412, 73, 265, 137, 1, 332, 204, 317, 376, 189, 248, 64, 44,
        273, 145, 476, 604, 276, 340, 404, 540, 328, 200, 65, 32, 257, 129, 380, 252, 108, 336, 208, 261, 133, 468, 669,
        605, 293, 165, 96, 320, 192, 652, 716, 524, 324, 196, 297, 169, 356, 228, 648, 712, 520, 596, 780, 653, 717,
        589, 289, 161, 360, 281, 153, 232, 776, 649, 713, 640, 512, 585, 704, 352, 781, 644, 516, 224, 708, 301, 173,
        777, 641, 577, 280, 344, 408, 532, 768, 656, 645, 709, 581, 528, 772, 705, 300, 364, 472, 1088, 600, 536, 661,
        597, 657, 773, 1152, 593, 769, 665, 601, 1216,
    ),
}
LONG_PLAN = {
    "share": 0.359375,
    "split": 1,
    "middle": ((0, 1, 0), (0, 1, 2), (0, 1, 3), (1, 0, 0), (1, 0, 2)),
    "via": {},
    "end": (
        157, 4, 185, 0, 177, 8, 156, 68, 1, 189, 64, 149, 12, 181, 72, 9, 153, 65, 5, 129, 76, 13, 152, 73, 376, 440,
        137, 45, 368, 69, 133, 432, 77, 37, 668, 141, 504, 380, 444, 144, 109, 32, 340, 496, 145, 372, 436, 101, 33,
        165, 508, 669, 40, 173, 96, 500, 320, 36, 512, 97, 328, 712, 520, 104, 41, 324, 516, 100, 44, 332, 524, 776,
        665, 404, 161, 105, 664, 716, 169, 108, 356, 708, 160, 468, 364, 1088, 704, 532, 780, 641, 705, 168, 772, 649,
        713, 768, 645, 709, 769, 653, 717, 777, 656, 1152, 773, 657, 781, 1216, 661,
    ),
    "inner": (
        5, 0, 4, 285, 157, 69, 1, 313, 185, 64, 8, 305, 177, 68, 284, 348, 412, 376, 248, 317, 189, 65, 13, 368, 240,
        277, 149, 72, 12, 309, 181, 476, 604, 9, 380, 281, 153, 252, 77, 540, 340, 45, 212, 257, 129, 372, 76, 244, 280,
        33, 344, 73, 265, 137, 408, 669, 605, 109, 37, 261, 133, 320, 192, 97, 32, 269, 141, 328, 200, 472, 536, 272,
        36, 324, 196, 101, 273, 145, 44, 332, 204, 96, 293, 165, 40, 665, 601, 100, 301, 173, 41, 600, 336, 108, 640,
        512, 400, 356, 228, 104, 648, 520, 704, 364, 236, 105, 644, 516, 708, 641, 577, 464, 652, 524, 705, 649, 585,
        768, 289, 161, 713, 645, 581, 772, 297, 169, 709, 653, 589, 769, 528, 288, 717, 592, 352, 777, 660, 532, 716,
        773, 296, 360, 1088, 712, 657, 593, 781, 661, 597, 1152, 780, 776, 1216,
    ),
}


def decode(step):
    step, side = divmod(step, 2)
    step, part = divmod(step, 2)
    step, k = divmod(step, PAIRS)
    step, cls = divmod(step, 2)
    op, field = divmod(step, 2)
    return op, field, cls, k, part, side


def load_groups(n):
    return [[i] for i in range(3)] + [list(range(i, min(i + 8, n))) for i in range(3, n, 8)]


def when(cond, do):
    if isinstance(cond, bool):
        if cond:
            do()
    else:
        pl.when(cond)(do)


def kernel(members, blocks, wide, plan, prior_hbm, post_hbm, control_hbm, relax_hbm, ocean_hbm, out,
           x, control, ocean, relax_ref, weights, total, y_in, v_in, v_sum, a_sum, a_in, b_sum, b_in, b_swap, spread, part1, part2, factors,
           sent_bytes, load_sem, control_sem, ocean_sem, relax_sem, sent, y_recv, v_recv, a_recv, b_recv, c_recv, w_recv,
           ga_recv, gb_recv, gy_recv, gv_recv, h_recv, m_recv):
    levels, columns = control.shape
    nblocks = levels // SUB
    pairs = nblocks // 2
    rest = columns - 2 * wide
    part_width = rest // plan["split"]
    half = part_width // 2
    depth = members // 2
    m = lax.axis_index("mem")
    hz = lax.axis_index("hz")
    z = lax.div(m, 2)
    y = lax.rem(m, 2)
    other = 1 - y
    upper = z >= depth // 2
    up = jnp.where(upper, 1, 0)
    inward = jnp.where(upper, z - 1, z + 1)
    outward = jnp.where(upper, z + 1, z - 1)
    distance = jnp.where(upper, depth - 1 - z, z)
    center = depth // 2 - 1
    to_in, to_out = up, 1 - up

    def device(zz, yy):
        return {"mem": zz * 2 + yy, "hz": hz}

    barrier = pltpu.get_barrier_semaphore()

    def greet(to):
        pl.semaphore_signal(barrier, inc=1, device_id=to, device_id_type=MESH)

    greet(device(z, other))
    greet(device(inward, y))
    pl.when(distance > 0)(lambda: greet(device(outward, y)))
    for i in range(1, blocks):
        greet({"mem": m, "hz": lax.rem(hz + i, blocks)})

    def block_of(k, side):
        return k + pairs * (up if side == NEAR else 1 - up)

    def rows(block):
        return pl.ds(pl.multiple_of(block * SUB, SUB), SUB)

    def wide_cols(yy):
        return pl.ds(pl.multiple_of(yy * wide, LANE), wide)

    def rest_cols(part):
        return pl.ds(2 * wide + part * part_width, part_width)

    fields = (post_hbm, prior_hbm)

    via_index = {chunk: i for i, chunk in enumerate(sorted(plan["via"]))}
    middle_index = {chunk: i for i, chunk in enumerate(plan["middle"])}

    ocean_load = pltpu.make_async_copy(ocean_hbm, ocean, ocean_sem)
    ocean_load.start()
    first_use = []
    for step in plan["end"]:
        op, field, cls, k, part, side = decode(step)
        if op < STAT1 and (field, k, side) not in first_use:
            first_use.append((field, k, side))
    groups = load_groups(len(first_use))
    group_of = {}
    for i, group in enumerate(groups):
        for n in group:
            field, k, side = first_use[n]
            block = block_of(k, side)
            group_of[first_use[n]] = i
            pltpu.make_async_copy(fields[field].at[0, rows(block)], x.at[field, rows(block)], load_sem.at[i]).start()
    control_load = pltpu.make_async_copy(control_hbm, control, control_sem)
    control_load.start()
    relax_load = pltpu.make_async_copy(relax_hbm, relax_ref, relax_sem)
    relax_load.start()
    pl.semaphore_wait(barrier, 1 + blocks + jnp.where(distance > 0, 1, 0))

    def arrive(dst, recv_sem):
        pltpu.make_async_remote_copy(src_ref=dst, dst_ref=dst, send_sem=sent, recv_sem=recv_sem,
                                     device_id=device(z, other), device_id_type=MESH).wait_recv()

    def merge(own, n_own, came, n_came, w, dst, field, block, scale=1.0):
        acc = jnp.zeros((SUB, LANE), jnp.float32)
        static = isinstance(n_own, int) and isinstance(n_came, int)
        equal = static and n_own == n_came
        if not static:
            f_own, f_came = (jnp.float32(n) if isinstance(n, int) else n.astype(jnp.float32) for n in (n_own, n_came))
        for j in range(own.shape[-1] // LANE):
            at = slice(j * LANE, (j + 1) * LANE)
            a, b = own[:, at], came[:, at]
            if equal:
                d = b - a
            elif static:
                d = b * float(n_own) - a * float(n_came)
            else:
                d = b * f_own - a * f_came
            acc += d * d * w[:, at]
            if dst is not None:
                dst[:, at] = a + b
        if equal:
            acc = acc * (scale / (2 * n_own))
        elif static:
            acc = acc * (scale / (n_own * n_came * (n_own + n_came)))
        else:
            acc = acc / jnp.full((SUB, LANE), f_own * f_came * (f_own + f_came), jnp.float32) * scale
        spread[field, block] += acc

    lane = lax.broadcasted_iota(jnp.int32, (SUB, LANE), 1)
    sub = lax.broadcasted_iota(jnp.int32, (SUB, LANE), 0)

    def role(order, end):
        pending = []
        loaded = set()
        finished = []
        state = {"factor": False, "weights": False}
        far = 0 if end else (1 if center == 1 else distance)
        at_center = False if end else (True if center == 1 else distance == center)
        before = False if end else (False if center == 1 else distance < center)
        last_step = {}
        for i, step in enumerate(order):
            op, *chunk = decode(step)
            if op in (AG_OUT, AGY_SEND):
                last_step[tuple(chunk)] = i

        def prepare():
            state["weights"] = True
            ocean_load.wait()
            weights[...] = jnp.broadcast_to(ocean[...].astype(jnp.float32), (SUB, columns))
            spread[...] = jnp.zeros_like(spread)

        def via(field, k, side):
            v = plan["via"].get((field, k, side), 0)
            return 0 if v == 0 else (1 if (v == 1) == end else 2)

        def own_count(field, k, side, here=True):
            v = via(field, k, side)
            return (2, 3, 1)[v] if here else (2, 1, 3)[v]

        def send(src, dst, recv_sem, to, cond=True):
            copy = pltpu.make_async_remote_copy(src_ref=src, dst_ref=dst, send_sem=sent, recv_sem=recv_sem,
                                                device_id=to, device_id_type=MESH)
            when(cond, copy.start)
            pending.append((cond, copy, src.size if hasattr(src, "size") else math.prod(src.shape)))

        def local(field, k, side):
            block = block_of(k, side)
            group = group_of[field, k, side]
            if group not in loaded:
                loaded.add(group)
                some = x.at[field, pl.ds(0, len(groups[group]) * SUB)]
                pltpu.make_async_copy(fields[field].at[0, pl.ds(0, len(groups[group]) * SUB)], some, load_sem.at[group]).wait()
            return block

        def chain_sem(field, cls, k, part, side, direction):
            if side == NEAR and direction is to_in and (field, cls, k) in middle_index:
                return c_recv.at[middle_index[field, cls, k], part]
            block = block_of(k, side)
            return a_recv.at[field, block] if cls == ROWS_FIRST else b_recv.at[field, block, part]

        def raw(field, block, cols):
            return x.at[field, rows(block), cols]

        def chain_send(field, cls, k, part, side, direction, to, cond=True):
            block = local(field, k, side)
            first = end and (side == FAR or (field, cls, k) in plan["middle"])
            if cls == ROWS_FIRST:
                src = raw(field, block, wide_cols(y)) if first and via(field, k, side) == 2 else a_sum.at[field, block]
                at, came = (field, block, direction), a_in
            else:
                src = raw(field, block, rest_cols(part)) if first else b_sum.at[field, block, part]
                at, came = (field, block, direction, part), b_in
            send(src, came.at[at], chain_sem(field, cls, k, part, side, direction), to, cond)

        def chain_merge(field, cls, k, part, side, direction, n_own, n_came, first, total_too=False):
            block = local(field, k, side)
            if cls == ROWS_FIRST:
                at = (field, block, direction)
                own = raw(field, block, wide_cols(y)) if first and via(field, k, side) == 2 else a_sum.at[field, block]
                into = a_sum.at[field, block]
                if total_too:
                    into = spot(cls, block, part) if field == POST else None
                arrive(a_in.at[at], chain_sem(field, cls, k, part, side, direction))
                merge(own, n_own, a_in.at[at], n_came, weights.at[:, wide_cols(y)], into, field, block)
            else:
                at = (field, block, direction, part)
                own = raw(field, block, rest_cols(part)) if first else b_sum.at[field, block, part]
                arrive(b_in.at[at], chain_sem(field, cls, k, part, side, direction))
                merge(own, n_own, b_in.at[at], n_came, weights.at[:, rest_cols(part)], b_sum.at[field, block, part], field, block)

        def spot(cls, block, part):
            return total.at[rows(block), wide_cols(y) if cls == ROWS_FIRST else rest_cols(part)]

        def total_sem(cls, block, part):
            return ga_recv.at[block] if cls == ROWS_FIRST else gb_recv.at[block, part]

        def total_send(cls, block, part, to, cond=True):
            send(spot(cls, block, part), spot(cls, block, part), total_sem(cls, block, part), to, cond)

        def total_arrive(cls, block, part):
            arrive(spot(cls, block, part), total_sem(cls, block, part))

        def half_send(block, yy, sem, to, cond=True):
            at = total.at[rows(block), wide_cols(yy)]
            send(at, at, sem, to, cond)

        def finish(block, cols):
            f = factors[block]
            c, p, t, o = (r.at[rows(block), cols] for r in (control, x.at[POST], total, out.at[0]))
            for j in range(c.shape[-1] // LANE):
                at = slice(j * LANE, (j + 1) * LANE)
                o[:, at] = c[:, at] + f * (p[:, at] - t[:, at] * (1.0 / members))

        def ready(block, cols):
            if state["factor"]:
                finish(block, cols)
            else:
                finished.append((block, cols))

        def do_step(i, step):
            op, field, cls, k, part, side = decode(step)
            if not state["weights"] and op in (Y_RECV, V_RECV, RS_FROM_OUT, RS_FROM_IN):
                prepare()
            if op < STAT1:
                middle = (field, cls, k) in plan["middle"]
                block = block_of(k, side)
                root_here = side == NEAR and end != middle
                here = True if end or not root_here else at_center
                rows_first = cls == ROWS_FIRST
                cols = wide_cols(y) if rows_first else rest_cols(part)
                v = via(field, k, side) if rows_first else 0
                chunk = (field, cls, k, part, side)
                if rows_first:
                    own, came = own_count(field, k, side), own_count(field, k, side, False)
                    out_count = 2 * far if v == 0 else came
                    end_count = 2 * (depth - 1) if v == 0 else 2 * depth - own
                    in_count, near_count = 2 * (depth - 1 - far), 2 * (far + 1)
                else:
                    own, out_count, end_count, in_count, near_count = 1, far, depth - 1, depth - 1 - far, far + 1
            if op == Y_SEND:
                local(field, k, side)
                src = v_sum.at[field, block] if v == 1 else raw(field, block, wide_cols(other))
                send(src, y_in.at[field, block], y_recv.at[field, block], device(z, other))
            elif op == Y_RECV:
                local(field, k, side)
                arrive(y_in.at[field, block], y_recv.at[field, block])
                merge(raw(field, block, wide_cols(y)), 1, y_in.at[field, block], 2 if v == 1 else 1, weights.at[:, wide_cols(y)],
                      a_sum.at[field, block], field, block)
            elif op == V_SEND:
                local(field, k, side)
                send(raw(field, block, wide_cols(other)), v_in.at[field, block], v_recv.at[via_index[field, k, side]],
                     device(inward if end else outward, y))
            elif op == V_RECV:
                local(field, k, side)
                arrive(v_in.at[field, block], v_recv.at[via_index[field, k, side]])
                merge(raw(field, block, wide_cols(other)), 1, v_in.at[field, block], 1, weights.at[:, wide_cols(other)],
                      v_sum.at[field, block], field, block)
            elif op == RS_IN:
                chain_send(*chunk, to_in, device(inward, y))
            elif op == RS_OUT:
                chain_send(*chunk, to_out, device(outward, y))
            elif op == RS_FROM_OUT:
                chain_merge(*chunk, to_in, own, out_count, True)
                if root_here and before is not False:
                    chain_send(*chunk, to_in, device(inward, y), before)
            elif op == RS_FROM_IN:
                if end:
                    chain_merge(*chunk, to_out, own, end_count, True, True)
                elif not middle:
                    chain_merge(*chunk, to_out, own, in_count, True)
                else:
                    when(here, lambda: chain_merge(*chunk, to_out, near_count, in_count, False, True))
                if rows_first and field == POST and root_here and before is False:
                    ready(block, cols)
            elif op == SW_SEND:
                at = (field, block, part)
                if field == POST:
                    send(b_sum.at[at], b_swap.at[at], w_recv.at[field, k, part], device(z, other), here)
                else:
                    send(b_sum.at[(*at, slice(None), pl.ds(pl.multiple_of(other * half, LANE), half))],
                         b_swap.at[(*at, slice(None), pl.ds(0, half))], w_recv.at[field, k, part], device(z, other), here)
            elif op == SW_RECV:
                at = (field, block, part)

                def swap():
                    if field == POST:
                        arrive(b_swap.at[at], w_recv.at[field, k, part])
                        merge(b_sum.at[at], depth, b_swap.at[at], depth, weights.at[:, rest_cols(part)], spot(cls, block, part),
                              field, block, 0.5)
                    else:
                        came = b_swap.at[(*at, slice(None), pl.ds(0, half))]
                        arrive(came, w_recv.at[field, k, part])
                        mine = pl.ds(pl.multiple_of(y * half, LANE), half)
                        place = pl.ds(pl.multiple_of(2 * wide + part * part_width + y * half, LANE), half)
                        merge(b_sum.at[(*at, slice(None), mine)], depth, came, depth, weights.at[:, place], None, field, block)

                when(here, swap)
                if field == POST and before is False:
                    ready(block, cols)
            elif op == AG_IN:
                total_send(cls, block, part, device(inward, y), here)
            elif op in (AG_OUT, AGY_SEND):
                if op == AG_OUT:
                    total_send(cls, block, part, device(outward, y), here)
                else:
                    half_send(block, y, gy_recv.at[block], device(z, other), here)
                if root_here and before is not False and last_step[chunk] == i:
                    when(before, lambda: total_arrive(cls, block, part))
                    total_send(cls, block, part, device(outward, y), before)
                    if rows_first:
                        half_send(block, y, gy_recv.at[block], device(z, other), before)
                    ready(block, cols)
            elif op == AG_RECV:
                total_arrive(cls, block, part)
                ready(block, cols)
            elif op in (AGY_RECV, W_RECV):
                sem = gy_recv.at[block] if op == AGY_RECV else gv_recv.at[via_index[field, k, side]]
                arrive(total.at[rows(block), wide_cols(other)], sem)
                ready(block, wide_cols(other))
            elif op == W_SEND:
                half_send(block, other, gv_recv.at[via_index[field, k, side]], device(inward if end else outward, y))
            elif op == STAT1:
                for field in (POST, PRIOR):
                    packed = jnp.zeros((SUB, LANE), jnp.float32)
                    for b in range(nblocks):
                        packed = jnp.where(lane == b, jnp.sum(spread[field, b], axis=1, keepdims=True), packed)
                    part1[hz, field] = packed
                for b in range(1, blocks):
                    send(part1.at[hz], part1.at[hz], h_recv, {"mem": m, "hz": lax.rem(hz + b, blocks)})
            elif op == STAT2:
                arrive(part1.at[pl.ds(0, blocks - 1)], h_recv)
                for field in (POST, PRIOR):
                    v = part1[0, field]
                    for b in range(1, blocks):
                        v = v + part1[b, field]
                    part2[m, field] = v
                for b in range(1, members):
                    send(part2.at[m], part2.at[m], m_recv, {"mem": lax.rem(m + b, members), "hz": hz})
            elif op == STAT3:
                arrive(part2.at[pl.ds(0, members - 1)], m_recv)
                sums = []
                for field in (POST, PRIOR):
                    v = part2[0, field]
                    for b in range(1, members):
                        v = v + part2[b, field]
                    sums.append(v)
                relax_load.wait()
                relax = jnp.zeros((SUB, LANE), jnp.float32)
                for level in range(levels):
                    relax = jnp.where((sub == level % SUB) & (lane == level // SUB), relax_ref[level], relax)
                factor = relax * (jnp.sqrt((sums[PRIOR] + eps) / (sums[POST] + eps)) - 1.0) + 1.0
                for b in range(nblocks):
                    factors[b] = jnp.broadcast_to(
                        jnp.sum(jnp.where(lane == b, factor, 0.0), axis=1, keepdims=True), (SUB, LANE))
                control_load.wait()
                state["factor"] = True
            if state["factor"] and finished:
                for _ in range(2):
                    if finished:
                        finish(*finished.pop(0))
        for i, step in enumerate(order):
            do_step(i, step)
        for todo in finished:
            finish(*todo)
        if all(isinstance(cond, bool) for cond, _, _ in pending):
            tiles = sum(size for cond, _, size in pending if cond) // (SUB * LANE)
            all_sent = sent_bytes.at[pl.ds(0, tiles * SUB)]
            pltpu.make_async_copy(all_sent, all_sent, sent).wait()
        else:
            for cond, copy, _ in pending:
                when(cond, copy.wait_send)

    @pl.when(distance == 0)
    def _():
        role(plan["end"], True)

    @pl.when(distance > 0)
    def _():
        role(plan["inner"], False)


def solution(mesh):
    members, blocks = mesh.shape["mem"], mesh.shape["hz"]
    plan = PLAN if members // 2 == SHORT_LINE else LONG_PLAN

    def on_device(prior, posterior, control, relax, ocean):
        levels, columns = control.shape
        n = levels // SUB
        wide = round(columns * plan["share"] / LANE) * LANE
        parts = plan["split"]
        rest = (columns - 2 * wide) // parts
        vmem = lambda *shape: pltpu.VMEM(shape, jnp.float32)
        dma = lambda *shape: pltpu.SemaphoreType.DMA(shape)
        one = pltpu.SemaphoreType.DMA
        return pl.pallas_call(
            functools.partial(kernel, members, blocks, wide, plan),
            out_shape=pltpu.VMEM(posterior.shape, jnp.float32),
            in_specs=[pl.BlockSpec(memory_space=pltpu.HBM)] * 5,
            out_specs=pl.BlockSpec(memory_space=pltpu.VMEM),
            scratch_shapes=[
                vmem(2, levels, columns), vmem(levels, columns), pltpu.VMEM((1, columns), jnp.int32),
                pltpu.SMEM((levels,), jnp.float32), vmem(SUB, columns), vmem(levels, columns),
                vmem(2, n, SUB, wide), vmem(2, n, SUB, wide), vmem(2, n, SUB, wide), vmem(2, n, SUB, wide),
                vmem(2, n, 2, SUB, wide), vmem(2, n, parts, SUB, rest), vmem(2, n, 2, parts, SUB, rest),
                vmem(2, n, parts, SUB, rest), vmem(2, n, SUB, LANE), vmem(blocks, 2, SUB, LANE),
                vmem(members, 2, SUB, LANE), vmem(n, SUB, LANE),
                vmem(4 * levels * columns // LANE, LANE),
                dma(len(load_groups(2 * n))), one, one, one, one, dma(2, n), dma(max(1, len(plan["via"]))), dma(2, n),
                dma(2, n, parts), dma(max(1, len(plan["middle"])), parts), dma(2, n // 2, parts),
                dma(n), dma(n, parts), dma(n), dma(max(1, len(plan["via"]))), one, one,
            ],
            compiler_params=pltpu.CompilerParams(
                collective_id=0, has_side_effects=True, vmem_limit_bytes=60 * 2**20
            ),
        )(prior, posterior, control, relax, ocean.reshape(1, columns))

    return jax.shard_map(
        on_device,
        mesh=mesh,
        in_specs=(P("mem", None, "hz"), P("mem", None, "hz"), P(None, "hz"), P(), P("hz")),
        out_specs=P("mem", None, "hz"),
        check_vma=False,
    )
```

time: 67.9 us -> 63.5 us (0.935)
  Pallas kernels: 66.4 us -> 62 us
    pallas_call x1, Pallas kernels: 66.4 us -> 62 us  [on_device(): pl.pallas_call(functools.partial(kernel, members, blocks, wide, plan), ou...]
where the time goes in v3:
time: 63.5 us; the launch traced here: 63.3 us
  Pallas kernels  62 us (98%)
  local copies, waits for them, and re-layouts  1.32 us (2%)
    pallas_call x1, Pallas kernels, on_device(): pl.pallas_call(functools.partial(kernel, members, blocks, wide, plan), ou...  62 us
    unnamed x1, local copies, waits for them, and re-layouts  1.32 us

profile of v3, /device:TPU:0, one launch (start us, length us, event | category | flops | bytes accessed | tf_op | source)
XLA Modules:
  0.0 63.3 jit_solution(17340108855636594988)
XLA Ops:
  0.0 62.0 %shard_map.55 = f32[1,64,8192]{2,1,0:T(8,128)S(1)} custom-call(f32[1,64,8192]{2,1,0:T(8,128)} %prior_hbm.1, f32[1,64,8192]{2,1,0:T(8,128)} %post_hbm.1, f32[64,8192]{1,0:T(8,128)} %control_hbm.1, f32[64]{0:T(128)} %relax_hbm.1, s32[1,8192]{1,0:T(1,128)} %bitcast.1), custom_call_target="tpu_custom_call" | custom-call | tf_op jit(solution)/shard_map/pallas_call | solution.py:483
  62.0 1.3 %copy.7 = f32[1,64,8192]{2,1,0:T(8,128)} copy(f32[1,64,8192]{2,1,0:T(8,128)S(1)} %shard_map.55) | data formatting | bytes 4194304

commit v4 on v3

--- a/solution.py
+++ b/solution.py
@@ -22,25 +22,25 @@
  AGY_SEND, AGY_RECV, V_SEND, V_RECV, W_SEND, W_RECV, STAT1, STAT2, STAT3) = range(20)
 
 PLAN = {
-    "share": 0.375,
+    "share": 0.390625,
     "split": 1,
-    "middle": ((0, 1, 1), (0, 1, 2), (0, 1, 3), (1, 0, 3)),
-    "via": {(1, 0, 1): 1, (1, 1, 0): 1, (1, 1, 1): 1, (1, 2, 0): 1, (1, 2, 1): 1, (1, 3, 1): 1},
+    "middle": ((0, 0, 0), (0, 1, 0), (1, 0, 3)),
+    "via": {(0, 1, 0): 2, (1, 0, 1): 1, (1, 1, 0): 1, (1, 1, 1): 1, (1, 2, 1): 1, (1, 3, 1): 1},
     "end": (
-        181, 13, 177, 5, 157, 149, 9, 77, 929, 141, 32, 69, 936, 185, 40, 156, 73, 937, 1, 137, 96, 933, 12, 189, 104,
-        941, 145, 37, 368, 148, 65, 432, 129, 932, 33, 76, 372, 133, 41, 101, 496, 165, 332, 8, 376, 97, 524, 4, 668,
-        105, 169, 0, 72, 328, 520, 380, 444, 336, 400, 68, 161, 45, 669, 64, 153, 508, 320, 704, 512, 464, 324, 708,
-        516, 109, 44, 173, 768, 660, 440, 436, 152, 772, 653, 717, 528, 108, 36, 172, 360, 504, 500, 649, 713, 781, 716,
-        352, 100, 356, 1088, 641, 705, 777, 645, 709, 1152, 780, 712, 664, 769, 1216, 661, 657, 773, 665, 776,
+        189, 1, 145, 8, 157, 149, 9, 181, 65, 937, 144, 13, 153, 72, 941, 177, 12, 73, 933, 137, 37, 77, 932, 141, 5,
+        129, 76, 929, 0, 348, 836, 101, 340, 41, 372, 69, 133, 380, 436, 40, 656, 64, 128, 368, 36, 344, 105, 169, 500,
+        33, 185, 328, 104, 520, 712, 657, 100, 165, 44, 332, 97, 161, 45, 640, 776, 524, 432, 408, 324, 108, 516, 404,
+        444, 641, 109, 412, 173, 496, 704, 472, 360, 536, 468, 376, 440, 508, 532, 32, 476, 540, 649, 172, 713, 768,
+        504, 356, 716, 96, 352, 1088, 705, 777, 653, 717, 780, 645, 1152, 709, 769, 1028, 665, 1216, 781, 661, 669, 773,
     ),
     "inner": (
-        865, 8, 872, 4, 873, 13, 309, 181, 72, 305, 177, 869, 12, 285, 68, 157, 877, 5, 277, 149, 372, 77, 9, 368, 240,
-        269, 141, 76, 868, 313, 0, 185, 69, 284, 348, 244, 412, 73, 265, 137, 1, 332, 204, 317, 376, 189, 248, 64, 44,
-        273, 145, 476, 604, 276, 340, 404, 540, 328, 200, 65, 32, 257, 129, 380, 252, 108, 336, 208, 261, 133, 468, 669,
-        605, 293, 165, 96, 320, 192, 652, 716, 524, 324, 196, 297, 169, 356, 228, 648, 712, 520, 596, 780, 653, 717,
-        589, 289, 161, 360, 281, 153, 232, 776, 649, 713, 640, 512, 585, 704, 352, 781, 644, 516, 224, 708, 301, 173,
-        777, 641, 577, 280, 344, 408, 532, 768, 656, 645, 709, 581, 528, 772, 705, 300, 364, 472, 1088, 600, 536, 661,
-        597, 657, 773, 1152, 593, 769, 665, 601, 1216,
+        873, 9, 877, 8, 869, 13, 317, 189, 73, 273, 145, 868, 44, 285, 157, 72, 277, 149, 865, 1, 380, 309, 181, 77,
+        272, 336, 400, 348, 220, 281, 153, 32, 108, 340, 212, 305, 177, 372, 244, 5, 65, 252, 265, 137, 464, 592, 344,
+        0, 528, 368, 240, 269, 96, 216, 141, 12, 257, 69, 129, 328, 200, 40, 657, 900, 64, 593, 4, 261, 133, 76, 332,
+        204, 256, 320, 704, 512, 576, 104, 297, 169, 68, 324, 196, 313, 185, 768, 641, 705, 577, 648, 520, 712, 360,
+        232, 293, 165, 376, 248, 289, 161, 769, 649, 713, 585, 652, 524, 716, 776, 356, 228, 644, 516, 708, 352, 224,
+        777, 301, 173, 653, 717, 589, 664, 780, 536, 660, 532, 645, 709, 581, 668, 772, 540, 964, 300, 364, 1088, 781,
+        665, 601, 661, 597, 773, 669, 1152, 605, 1216,
     ),
 }
 LONG_PLAN = {
@@ -91,7 +91,7 @@
 def kernel(members, blocks, wide, plan, prior_hbm, post_hbm, control_hbm, relax_hbm, ocean_hbm, out,
            x, control, ocean, relax_ref, weights, total, y_in, v_in, v_sum, a_sum, a_in, b_sum, b_in, b_swap, spread, part1, part2, factors,
            sent_bytes, load_sem, control_sem, ocean_sem, relax_sem, sent, y_recv, v_recv, a_recv, b_recv, c_recv, w_recv,
-           ga_recv, gb_recv, gy_recv, gv_recv, h_recv, m_recv):
+           gy_recv, h_recv, m_recv):
     levels, columns = control.shape
     nblocks = levels // SUB
     pairs = nblocks // 2
@@ -280,7 +280,7 @@
             return total.at[rows(block), wide_cols(y) if cls == ROWS_FIRST else rest_cols(part)]
 
         def total_sem(cls, block, part):
-            return ga_recv.at[block] if cls == ROWS_FIRST else gb_recv.at[block, part]
+            return a_recv.at[POST, block] if cls == ROWS_FIRST else b_recv.at[POST, block, part]
 
         def total_send(cls, block, part, to, cond=True):
             send(spot(cls, block, part), spot(cls, block, part), total_sem(cls, block, part), to, cond)
@@ -292,14 +292,25 @@
             at = total.at[rows(block), wide_cols(yy)]
             send(at, at, sem, to, cond)
 
+        def tiles(width):
+            for j in range(0, width // LANE, 8):
+                yield [slice(i * LANE, (i + 1) * LANE) for i in range(j, min(j + 8, width // LANE))]
+
+        def anomaly(block, cols):
+            p, t, o = (r.at[rows(block), cols] for r in (x.at[POST], total, out.at[0]))
+            for some in tiles(o.shape[-1]):
+                for at, v in [(at, p[:, at] - t[:, at] * (1.0 / members)) for at in some]:
+                    o[:, at] = v
+
         def finish(block, cols):
             f = factors[block]
-            c, p, t, o = (r.at[rows(block), cols] for r in (control, x.at[POST], total, out.at[0]))
-            for j in range(c.shape[-1] // LANE):
-                at = slice(j * LANE, (j + 1) * LANE)
-                o[:, at] = c[:, at] + f * (p[:, at] - t[:, at] * (1.0 / members))
+            c, o = control.at[rows(block), cols], out.at[0, rows(block), cols]
+            for some in tiles(o.shape[-1]):
+                for at, v in [(at, c[:, at] + f * o[:, at]) for at in some]:
+                    o[:, at] = v
 
         def ready(block, cols):
+            anomaly(block, cols)
             if state["factor"]:
                 finish(block, cols)
             else:
@@ -402,11 +413,11 @@
                 total_arrive(cls, block, part)
                 ready(block, cols)
             elif op in (AGY_RECV, W_RECV):
-                sem = gy_recv.at[block] if op == AGY_RECV else gv_recv.at[via_index[field, k, side]]
+                sem = gy_recv.at[block] if op == AGY_RECV else v_recv.at[via_index[field, k, side]]
                 arrive(total.at[rows(block), wide_cols(other)], sem)
                 ready(block, wide_cols(other))
             elif op == W_SEND:
-                half_send(block, other, gv_recv.at[via_index[field, k, side]], device(inward if end else outward, y))
+                half_send(block, other, v_recv.at[via_index[field, k, side]], device(inward if end else outward, y))
             elif op == STAT1:
                 for field in (POST, PRIOR):
                     packed = jnp.zeros((SUB, LANE), jnp.float32)
@@ -415,6 +426,12 @@
                     part1[hz, field] = packed
                 for b in range(1, blocks):
                     send(part1.at[hz], part1.at[hz], h_recv, {"mem": m, "hz": lax.rem(hz + b, blocks)})
+                relax_load.wait()
+                relax = jnp.zeros((SUB, LANE), jnp.float32)
+                for level in range(levels):
+                    relax = jnp.where((sub == level % SUB) & (lane == level // SUB), relax_ref[level], relax)
+                state["relax"] = relax
+                control_load.wait()
             elif op == STAT2:
                 arrive(part1.at[pl.ds(0, blocks - 1)], h_recv)
                 for field in (POST, PRIOR):
@@ -432,15 +449,11 @@
                     for b in range(1, members):
                         v = v + part2[b, field]
                     sums.append(v)
-                relax_load.wait()
-                relax = jnp.zeros((SUB, LANE), jnp.float32)
-                for level in range(levels):
-                    relax = jnp.where((sub == level % SUB) & (lane == level // SUB), relax_ref[level], relax)
+                relax = state["relax"]
                 factor = relax * (jnp.sqrt((sums[PRIOR] + eps) / (sums[POST] + eps)) - 1.0) + 1.0
                 for b in range(nblocks):
                     factors[b] = jnp.broadcast_to(
                         jnp.sum(jnp.where(lane == b, factor, 0.0), axis=1, keepdims=True), (SUB, LANE))
-                control_load.wait()
                 state["factor"] = True
             if state["factor"] and finished:
                 for _ in range(2):
@@ -495,7 +508,7 @@
                 vmem(4 * levels * columns // LANE, LANE),
                 dma(len(load_groups(2 * n))), one, one, one, one, dma(2, n), dma(max(1, len(plan["via"]))), dma(2, n),
                 dma(2, n, parts), dma(max(1, len(plan["middle"])), parts), dma(2, n // 2, parts),
-                dma(n), dma(n, parts), dma(n), dma(max(1, len(plan["via"]))), one, one,
+                dma(n), one, one,
             ],
             compiler_params=pltpu.CompilerParams(
                 collective_id=0, has_side_effects=True, vmem_limit_bytes=60 * 2**20

time: 63.5 us -> 63 us (level)
  no operation moved by 1% of the time
where the time goes in v4:
time: 63 us; the launch traced here: 62.9 us
  Pallas kernels  61.5 us (98%)
  local copies, waits for them, and re-layouts  1.32 us (2%)
    pallas_call x1, Pallas kernels, on_device(): pl.pallas_call(functools.partial(kernel, members, blocks, wide, plan), ou...  61.5 us
    unnamed x1, local copies, waits for them, and re-layouts  1.32 us

profile of v4, /device:TPU:0, one launch (start us, length us, event | category | flops | bytes accessed | tf_op | source)
XLA Modules:
  0.0 62.9 jit_solution(6173705437125074096)
XLA Ops:
  0.0 61.5 %shard_map.55 = f32[1,64,8192]{2,1,0:T(8,128)S(1)} custom-call(f32[1,64,8192]{2,1,0:T(8,128)} %prior_hbm.1, f32[1,64,8192]{2,1,0:T(8,128)} %post_hbm.1, f32[64,8192]{1,0:T(8,128)} %control_hbm.1, f32[64]{0:T(128)} %relax_hbm.1, s32[1,8192]{1,0:T(1,128)} %bitcast.1), custom_call_target="tpu_custom_call" | custom-call | tf_op jit(solution)/shard_map/pallas_call | solution.py:496
  61.5 1.3 %copy.7 = f32[1,64,8192]{2,1,0:T(8,128)} copy(f32[1,64,8192]{2,1,0:T(8,128)S(1)} %shard_map.55) | data formatting | bytes 4194304
